TPU v7x, 32 devices: a whole 2x2x4 slice. The times are simulated.
32 devices in a mesh: sfc: 8 (over z, y), sub: 4 (over x, core).
Axes of the slice: x: 2, y: 2, z: 4, core: 2. Of those that a mesh axis runs over, the one named last changes fastest.
Arguments:
- vectors: float32 [64, 512, 256], P(None, ('sfc', 'sub')), may hold values from -10 to 10
- reaction: float32 [512, 256], P(('sfc', 'sub')), may hold values from 0.5 to 5
Outputs:
- basis: float32 [64, 512, 256], P(None, ('sfc', 'sub'))
- upper: float32 [64, 64], replicated
All inputs are finite; a program needn't handle non-finite values.
Results may differ from a plain program's by a relative error of at most 0.0003.
Values sent between devices are 32-bit elements; how exact they have to be, the bound alone decides.
A program may use at most 64 MiB of HBM per device.

v0:
```python
import math

import jax
import jax.numpy as jnp
from jax import lax
from jax.sharding import PartitionSpec as P

NY = 32
NL = 8
POWERS = 3


DELTA_MASS = 0.5


def with_halo(cells, sides, width):
    for axis, dim in sides:
        count = lax.axis_size(axis)
        ends = count - 1
        head = lax.slice_in_dim(cells, 0, width, axis=dim)
        tail = lax.slice_in_dim(cells, cells.shape[dim] - width, cells.shape[dim], axis=dim)
        cells = jnp.concatenate(
            [
                lax.ppermute(tail, axis, [(i, (i + 1) % count) for i in range(ends)]),
                cells,
                lax.ppermute(head, axis, [((i + 1) % count, i) for i in range(ends)]),
            ],
            axis=dim,
        )
    return cells


def line_tables(count):
    index = jnp.arange(count)
    offset = index[:, None] - index[None, :]
    near = (jnp.abs(offset) == 1).astype(jnp.float32)
    same = (offset == 0).astype(jnp.float32)
    mass = (4.0 * same + near) / 6.0
    stiff = 2.0 * same - near
    return (mass, stiff)


def tables(across, layers):
    mass_across, stiff_across = line_tables(across)
    mass_layers, stiff_layers = line_tables(layers)
    mass_plane = jnp.kron(mass_layers, mass_across)
    stiff_plane = (
        jnp.kron(mass_layers, stiff_across)
        + jnp.kron(stiff_layers, mass_across)
        + DELTA_MASS * mass_plane
    )
    return jnp.concatenate([mass_plane, stiff_plane], axis=1)


def plane_products(field, table):
    plane = table.shape[0]
    both = jnp.einsum("kzp,pq->kzq", field, table, precision=lax.Precision.HIGHEST)
    return (both[..., :plane], both[..., plane:])


def operate(field, reaction, table):
    massed, mixed = plane_products(field, table)
    edge_term = mixed / 6.0 - massed
    padded = with_halo(edge_term, ((("sfc", "sub"), 1),), 1)
    neighbours = padded[:, :-2] + padded[:, 2:]
    return neighbours + 4.0 / 6.0 * mixed + 2.0 * massed + reaction[None] * field


def whole_factor(local):
    gram = jnp.dot(local, local.T, precision=lax.Precision.HIGHEST)
    total = lax.psum(gram, ("sfc", "sub"))
    return jnp.linalg.cholesky(total)


def lower_solve(lower, block):
    return lax.linalg.triangular_solve(lower, block, left_side=True, lower=True)


def per_device(vectors, reaction):
    table = tables(NY, NL)
    field = vectors
    for _ in range(POWERS):
        field = operate(field, reaction, table)
    local = field.reshape(field.shape[0], -1)
    lower_one = whole_factor(local)
    first = lower_solve(lower_one, local)
    lower_two = whole_factor(first)
    second = lower_solve(lower_two, first)
    scale = math.sqrt(lax.axis_size("sfc") * lax.axis_size("sub") * local.shape[1])
    upper = jnp.dot(lower_one, lower_two, precision=lax.Precision.HIGHEST).T / scale
    return ((second * scale).reshape(vectors.shape), upper)


def solution(mesh):
    placed = (P(None, ("sfc", "sub"), None), P(("sfc", "sub"), None))
    return jax.shard_map(
        per_device,
        mesh=mesh,
        in_specs=placed,
        out_specs=(P(None, ("sfc", "sub"), None), P()),
        check_vma=False,
    )
```

profile of v0, /device:TPU:0, one launch (start us, length us, event | category | flops | bytes accessed | tf_op | source)
XLA Modules:
  0.0 152.5 jit_solution(1561632378919360733)
XLA Ops:
  0.7 0.3 broadcast_multiply_fusion
  1.0 0.0 copy-start
  1.0 0.3 mul.143
  1.3 0.3 add.78
  1.6 0.5 copy-done
  2.2 2.3 %convolution_bitcast_fusion = f32[64,16,512]{2,0,1:T(8,128)S(1)} fusion(f32[64,16,256]{2,1,0:T(8,128)S(1)} %copy-done, f32[256,256]{1,0:T(8,128)S(1)} %multiply_add_fusion.1, f32[256,256]{1,0:T(8,128)S(1)} %mul.143), kind=kOutput, calls=%fused_computation.1 | convolution fusion | flops 1610743808 | bytes 3670016 | tf_op jit(solution)/shard_map/kzp,pq->kzq/dot_general | solution.py:57
  4.5 0.0 copy-start.1
  4.5 0.2 multiply_subtract_fusion.2
  4.7 2.4 %collective-permute-start = (f32[64,1,256]{2,0,1:T(8,128)S(1)}, f32[64,1,256]{2,0,1:T(8,128)S(1)}, u32[]{:S(2)}, u32[]{:S(2)}) collective-permute-start(f32[64,1,256]{2,0,1:T(8,128)S(1)} %get-tuple-element.8), channel_id=1, source_target_pairs={{0,1},{1,2},{2,3},{3,4},{4,5},{5,6},{6,7},{7,8},{8,9},{9,10},{10,1... | collective-permute-start | bytes 196616 | tf_op jit(solution)/shard_map/ppermute | solution.py:24
  7.1 1.3 collective-permute-start.1
  8.4 0.0 collective-permute-done
  8.4 3.9 %collective-permute-done.1 = f32[64,1,256]{2,0,1:T(8,128)S(1)} collective-permute-done((f32[64,1,256]{2,0,1:T(8,128)S(1)}, f32[64,1,256]{2,0,1:T(8,128)S(1)}, u32[]{:S(2)}, u32[]{:S(2)}) %collective-permute-start.1) | collective-permute-done | bytes 65568 | tf_op jit(solution)/shard_map/ppermute | solution.py:26
  12.3 0.0 copy-done.1
  12.3 0.8 fusion.11
  13.2 1.8 %fusion.14 = f32[64,16,512]{2,0,1:T(8,128)S(1)} fusion(f32[64,16,256]{2,0,1:T(8,128)S(1)} %fusion.11, f32[256,256]{1,0:T(8,128)S(1)} %multiply_add_fusion.1, f32[256,256]{1,0:T(8,128)S(1)} %mul.143), kind=kOutput, calls=%fused_computation.30 | convolution fusion | flops 1610743808 | bytes 3670016 | tf_op jit(solution)/shard_map/kzp,pq->kzq/dot_general | solution.py:57
  15.0 0.2 multiply_subtract_fusion.1
  15.2 4.8 %collective-permute-start.2 = (f32[64,1,256]{2,0,1:T(8,128)S(1)}, f32[64,1,256]{2,0,1:T(8,128)S(1)}, u32[]{:S(2)}, u32[]{:S(2)}) collective-permute-start(f32[64,1,256]{2,0,1:T(8,128)S(1)} %get-tuple-element.6), channel_id=1, source_target_pairs={{0,1},{1,2},{2,3},{3,4},{4,5},{5,6},{6,7},{7,8},{8,9},{9,10},{10,1... | collective-permute-start | bytes 196616 | tf_op jit(solution)/shard_map/ppermute | solution.py:24
  20.0 1.3 collective-permute-start.3
  21.3 0.0 collective-permute-done.2
  21.4 1.8 %collective-permute-done.3 = f32[64,1,256]{2,0,1:T(8,128)S(1)} collective-permute-done((f32[64,1,256]{2,0,1:T(8,128)S(1)}, f32[64,1,256]{2,0,1:T(8,128)S(1)}, u32[]{:S(2)}, u32[]{:S(2)}) %collective-permute-start.3) | collective-permute-done | bytes 65568 | tf_op jit(solution)/shard_map/ppermute | solution.py:26
  23.2 0.3 fusion.7
  23.5 1.8 %fusion.13 = f32[64,16,512]{2,0,1:T(8,128)S(1)} fusion(f32[64,16,256]{2,0,1:T(8,128)S(1)} %fusion.7, f32[256,256]{1,0:T(8,128)S(1)} %multiply_add_fusion.1, f32[256,256]{1,0:T(8,128)S(1)} %mul.143), kind=kOutput, calls=%fused_computation.29 | convolution fusion | flops 1610743808 | bytes 3670016 | tf_op jit(solution)/shard_map/kzp,pq->kzq/dot_general | solution.py:57
  25.4 0.2 multiply_subtract_fusion
  25.6 5.1 %collective-permute-start.4 = (f32[64,1,256]{2,0,1:T(8,128)S(1)}, f32[64,1,256]{2,0,1:T(8,128)S(1)}, u32[]{:S(2)}, u32[]{:S(2)}) collective-permute-start(f32[64,1,256]{2,0,1:T(8,128)S(1)} %get-tuple-element.4), channel_id=1, source_target_pairs={{0,1},{1,2},{2,3},{3,4},{4,5},{5,6},{6,7},{7,8},{8,9},{9,10},{10,1... | collective-permute-start | bytes 196616 | tf_op jit(solution)/shard_map/ppermute | solution.py:24
  30.7 1.3 collective-permute-start.5
  32.0 0.0 collective-permute-done.4
  32.0 1.8 %collective-permute-done.5 = f32[64,1,256]{2,0,1:T(8,128)S(1)} collective-permute-done((f32[64,1,256]{2,0,1:T(8,128)S(1)}, f32[64,1,256]{2,0,1:T(8,128)S(1)}, u32[]{:S(2)}, u32[]{:S(2)}) %collective-permute-start.5) | collective-permute-done | bytes 65568 | tf_op jit(solution)/shard_map/ppermute | solution.py:26
  33.8 0.3 fusion.3
  34.1 1.0 convolution_bitcast_fusion.1
  35.1 45.9 %psum.14 = f32[64,64]{0,1:T(8,128)S(1)} all-reduce(f32[64,64]{0,1:T(8,128)S(1)} %convolution_bitcast_fusion.1), channel_id=1, replica_groups=mesh['sfc'=8,'sub'=4] {'sfc','sub'}, use_global_device_ids=true, to_apply=%region_0.1 | all-reduce | flops 4096 | bytes 32768 | tf_op jit(solution)/shard_map/psum | solution.py:71
  81.0 0.1 copy.25
  81.1 5.8 %cholesky.44 = f32[64,64]{1,0:T(8,128)S(1)} custom-call(f32[64,64]{1,0:T(8,128)S(1)} %fusion.19), custom_call_target="Cholesky" | custom-call | tf_op jit(solution)/shard_map/jit(cholesky)/cholesky | solution.py:72
  87.0 0.6 compare_reduce_fusion.1
  87.6 0.7 fusion.23
  88.3 4.9 %custom-call.6 = f32[1,64,64]{1,2,0:T(8,128)S(1)} custom-call(f32[1,64,64]{2,1,0:T(8,128)S(1)} %fusion.23), custom_call_target="InvertDiagBlocksLowerTriangular" | custom-call | tf_op jit(solution)/shard_map/triangular_solve/custom-call.0 | solution.py:76
  93.2 0.1 copy.36
  93.3 1.0 fusion.17
  94.3 1.0 fusion.44
  95.3 40.3 %psum.15 = f32[64,64]{0,1:T(8,128)S(1)} all-reduce(f32[64,64]{0,1:T(8,128)S(1)} %fusion.44), channel_id=1, replica_groups=mesh['sfc'=8,'sub'=4] {'sfc','sub'}, use_global_device_ids=true, to_apply=%region_3.6 | all-reduce | flops 4096 | bytes 32768 | tf_op jit(solution)/shard_map/psum | solution.py:71
  135.6 0.1 copy.28
  135.7 5.8 %cholesky.55 = f32[64,64]{1,0:T(8,128)S(1)} custom-call(f32[64,64]{1,0:T(8,128)S(1)} %fusion.16), custom_call_target="Cholesky" | custom-call | tf_op jit(solution)/shard_map/jit(cholesky)/cholesky | solution.py:72
  141.6 0.7 compare_reduce_fusion
  142.3 2.2 %convolution_multiply_fusion.1 = f32[64,64]{1,0:T(8,128)} fusion(f32[64,64]{1,0:T(8,128)S(1)} %cholesky.55, f32[64,64]{1,0:T(8,128)S(1)} %cholesky.44, pred[]{:T(512)} %compare_reduce_fusion, pred[]{:T(512)} %compare_reduce_fusion.1), kind=kOutput, calls=%fused_computation.2 | convolution fusion | flops 3174400 | bytes 49154 | tf_op jit(solution)/shard_map/dot_general | solution.py:90
  144.5 0.7 select_bitcast_fusion
  145.2 4.9 %custom-call.7 = f32[1,64,64]{1,2,0:T(8,128)S(1)} custom-call(f32[1,64,64]{2,1,0:T(8,128)S(1)} %select_bitcast_fusion), custom_call_target="InvertDiagBlocksLowerTriangular" | custom-call | tf_op jit(solution)/shard_map/triangular_solve/custom-call.0 | solution.py:76
  150.1 1.1 convolution_multiply_fusion
  151.2 1.3 copy.37
  (10 shorter events, 0.2 us)
Async XLA Ops:
  1.0 1.2 copy-start
  4.5 7.8 %copy-start.1 = (f32[16,256]{1,0:T(8,128)S(1)}, f32[16,256]{1,0:T(8,128)}, u32[]{:S(2)}) copy-start(f32[16,256]{1,0:T(8,128)} %param.6) | copy-start | bytes 49156
  4.7 3.7 %collective-permute-start = (f32[64,1,256]{2,0,1:T(8,128)S(1)}, f32[64,1,256]{2,0,1:T(8,128)S(1)}, u32[]{:S(2)}, u32[]{:S(2)}) collective-permute-start(f32[64,1,256]{2,0,1:T(8,128)S(1)} %get-tuple-element.8), channel_id=1, source_target_pairs={{0,1},{1,2},{2,3},{3,4},{4,5},{5,6},{6,7},{7,8},{8,9},{9,10},{10,1... | collective-permute-start | bytes 196616 | tf_op jit(solution)/shard_map/ppermute | solution.py:24
  7.1 5.2 %collective-permute-start.1 = (f32[64,1,256]{2,0,1:T(8,128)S(1)}, f32[64,1,256]{2,0,1:T(8,128)S(1)}, u32[]{:S(2)}, u32[]{:S(2)}) collective-permute-start(f32[64,1,256]{2,0,1:T(8,128)S(1)} %get-tuple-element.9), channel_id=1, source_target_pairs={{1,0},{2,1},{3,2},{4,3},{5,4},{6,5},{7,6},{8,7},{9,8},{10,9},{11,1... | collective-permute-start | bytes 196616 | tf_op jit(solution)/shard_map/ppermute | solution.py:26
  15.2 6.2 %collective-permute-start.2 = (f32[64,1,256]{2,0,1:T(8,128)S(1)}, f32[64,1,256]{2,0,1:T(8,128)S(1)}, u32[]{:S(2)}, u32[]{:S(2)}) collective-permute-start(f32[64,1,256]{2,0,1:T(8,128)S(1)} %get-tuple-element.6), channel_id=1, source_target_pairs={{0,1},{1,2},{2,3},{3,4},{4,5},{5,6},{6,7},{7,8},{8,9},{9,10},{10,1... | collective-permute-start | bytes 196616 | tf_op jit(solution)/shard_map/ppermute | solution.py:24
  20.0 3.1 %collective-permute-start.3 = (f32[64,1,256]{2,0,1:T(8,128)S(1)}, f32[64,1,256]{2,0,1:T(8,128)S(1)}, u32[]{:S(2)}, u32[]{:S(2)}) collective-permute-start(f32[64,1,256]{2,0,1:T(8,128)S(1)} %get-tuple-element.7), channel_id=1, source_target_pairs={{1,0},{2,1},{3,2},{4,3},{5,4},{6,5},{7,6},{8,7},{9,8},{10,9},{11,1... | collective-permute-start | bytes 196616 | tf_op jit(solution)/shard_map/ppermute | solution.py:26
  25.6 6.4 %collective-permute-start.4 = (f32[64,1,256]{2,0,1:T(8,128)S(1)}, f32[64,1,256]{2,0,1:T(8,128)S(1)}, u32[]{:S(2)}, u32[]{:S(2)}) collective-permute-start(f32[64,1,256]{2,0,1:T(8,128)S(1)} %get-tuple-element.4), channel_id=1, source_target_pairs={{0,1},{1,2},{2,3},{3,4},{4,5},{5,6},{6,7},{7,8},{8,9},{9,10},{10,1... | collective-permute-start | bytes 196616 | tf_op jit(solution)/shard_map/ppermute | solution.py:24
  30.7 3.1 %collective-permute-start.5 = (f32[64,1,256]{2,0,1:T(8,128)S(1)}, f32[64,1,256]{2,0,1:T(8,128)S(1)}, u32[]{:S(2)}, u32[]{:S(2)}) collective-permute-start(f32[64,1,256]{2,0,1:T(8,128)S(1)} %get-tuple-element.5), channel_id=1, source_target_pairs={{1,0},{2,1},{3,2},{4,3},{5,4},{6,5},{7,6},{8,7},{9,8},{10,9},{11,1... | collective-permute-start | bytes 196616 | tf_op jit(solution)/shard_map/ppermute | solution.py:26
where the time goes:
time: 153 us; the launch traced here: 152 us
  blocking collectives  86.2 us (56%)
  other arithmetic  26.6 us (17%)
  starting transfers between devices  16.2 us (11%)
  matrix products  12.2 us (8%)
  waiting for transfers between devices  7.62 us (5%)
  local copies, waits for them, and re-layouts  2.74 us (2%)
    psum x2, blocking collectives, whole_factor(): total = lax.psum(gram, ('sfc', 'sub'))  86.2 us
    another operation x6, other arithmetic, whole_factor(): return jnp.linalg.cholesky(total)  13.1 us
    ppermute x3, starting transfers between devices, with_halo(): lax.ppermute(tail, axis, [(i, (i + 1) % count) for i in range(ends)])  12.4 us
    another operation x4, other arithmetic, lower_solve(): return lax.linalg.triangular_solve(lower, block, left_side=True, lower=True)  11.1 us
    ppermute x3, waiting for transfers between devices, with_halo(): lax.ppermute(head, axis, [((i + 1) % count, i) for i in range(ends)])  7.61 us
    dot_general x3, matrix products, plane_products(): jnp.einsum('kzp,pq->kzq', field, table, precision=lax.Precision.HIGHEST)  5.98 us
    ppermute x3, starting transfers between devices, with_halo(): lax.ppermute(head, axis, [((i + 1) % count, i) for i in range(ends)])  3.88 us
  transfers between devices with their start and end apart: 6, of which 3 were waited for; matrix products, arithmetic and copies ran while one was open for 0% of the time, Pallas kernels for 0%

commit v1 on v0

v1 whole, which is shorter than its diff:
```python
import functools
import math

import jax
import jax.numpy as jnp
import numpy as np
from jax import lax
from jax.experimental import pallas as pl
from jax.experimental.pallas import tpu as pltpu
from jax.sharding import PartitionSpec as P

NY = 32
NL = 8
POWERS = 3

MESH = pl.DeviceIdType.MESH
F32 = jnp.float32
BF16 = jnp.bfloat16
STEP = 4
LANES = 128


def plane_table(across, layers):
    def near(n):
        return np.eye(n, k=1) + np.eye(n, k=-1)

    one_a, one_l = np.eye(across), np.eye(layers)
    same = np.kron(one_l, one_a)
    side = np.kron(one_l, near(across)) + np.kron(near(layers), one_a)
    corner = np.kron(near(layers), near(across))
    edge = 16.0 * same - 68.0 * side - 35.0 * corner
    own = 304.0 * same + 4.0 * side - 17.0 * corner
    return np.concatenate([edge, own], axis=1)


def split3(x):
    high = x.astype(BF16)
    rest = x - high.astype(F32)
    mid = rest.astype(BF16)
    low = (rest - mid.astype(F32)).astype(BF16)
    return high, mid, low


def loop(count, body):
    if count <= 16:
        for i in range(count):
            body(i)
    else:
        lax.fori_loop(0, count, lambda i, c: (body(i), c)[1], 0)


def gram_of(slabs):
    k = slabs[0].shape[0]
    wide = jnp.concatenate([jnp.concatenate(split3(s), axis=0) for s in slabs], axis=1)
    pairs = lax.dot_general(wide, wide, (((1,), (1,)), ((), ())), preferred_element_type=F32)
    total = None
    for i in (2, 1, 0):
        for j in (2, 1, 0):
            term = pairs[i * k : (i + 1) * k, j * k : (j + 1) * k]
            total = term if total is None else total + term
    return total


def left_parts(matrix):
    a, b, c = split3(matrix)
    return jnp.concatenate([a, a, a, b, b, c], axis=1)


def left_apply(parts, slab):
    a, b, c = split3(slab)
    stacked = jnp.concatenate([a, b, c, a, b, a], axis=0)
    return jnp.dot(parts, stacked, preferred_element_type=F32)


def eliminate(gram):
    k = gram.shape[0]
    rows = lax.broadcasted_iota(jnp.int32, (k, 2 * k), 0)
    cols = lax.broadcasted_iota(jnp.int32, (k, 2 * k), 1)
    unit = (rows + k == cols).astype(F32)
    work = jnp.concatenate([gram, unit[:, k:]], axis=1)
    for start in range(0, k, STEP):
        base = start // 8 * 8
        done, live = work[:base], work[base:]
        live_rows = rows[base:]
        n = live.shape[0]
        columns = [jnp.broadcast_to(live[:, start + i : start + i + 1], (n, 2 * k)) for i in range(STEP)]
        for i in range(STEP):
            j = start + i
            at = j - base
            pivot = columns[i][at : at + 1, :]
            factor = jnp.where(live_rows > j, columns[i] * (1.0 / pivot), 0.0)
            for later in range(i + 1, STEP):
                columns[later] = columns[later] - factor * columns[later][at : at + 1, :]
            live = live - factor * live[at : at + 1, :]
        work = live if base == 0 else jnp.concatenate([done, live], axis=0)
    diagonal = jnp.sum(jnp.where(rows == cols, work, 0.0), axis=1, keepdims=True)
    root = lax.rsqrt(diagonal)
    root = root * (1.5 - 0.5 * diagonal * root * root)
    upper = jnp.where(cols >= rows, work, 0.0)[:, :k] * (1.0 / (diagonal * root))
    inverse = work[:, k:] * root
    return upper, inverse


def pack(gram):
    half = gram.shape[0] // 2
    return jnp.concatenate([gram[:half], gram[half:]], axis=1)


def unpack(packed):
    k = packed.shape[1] // 2
    return jnp.concatenate([packed[:, :k], packed[:, k:]], axis=0)


def gather_sum(axis, box, send_sem, recv_sem, value):
    count = lax.axis_size(axis)
    me = lax.axis_index(axis)
    box[me] = value

    def copy(i, slot, target):
        return pltpu.make_async_remote_copy(
            src_ref=box.at[slot],
            dst_ref=box.at[slot],
            send_sem=send_sem.at[i],
            recv_sem=recv_sem.at[slot],
            device_id={axis: target},
            device_id_type=MESH,
        )

    def start(i):
        copy(i, me, lax.rem(me + i + 1, count)).start()

    def take(i):
        other = lax.rem(me + i + 1, count)
        copy(i, other, other).wait_recv()

    def sent(i):
        copy(i, me, lax.rem(me + i + 1, count)).wait_send()

    loop(count - 1, start)
    loop(count - 1, take)
    if count <= 16:
        total = box[0]
        for i in range(1, count):
            total = total + box[i]
    else:
        total = lax.fori_loop(1, count, lambda i, t: t + box[i], box[0])
    return total, lambda: loop(count - 1, sent)


def main_kernel(
    vec_ref, react_ref, table_ref, q_ref, upper_ref, gram_ref,
    raw, react, fields, edges, send_l, send_r, from_l, from_r,
    box_sub1, box_sfc1, box_sub2, box_sfc2,
    in_sem, halo_send, halo_recv,
    ss1, rs1, sf1, rf1, ss2, rs2, sf2, rf2,
):
    width = POWERS
    n_sfc, n_sub = lax.axis_size("sfc"), lax.axis_size("sub")
    p_sfc, p_sub = lax.axis_index("sfc"), lax.axis_index("sub")
    me = p_sfc * n_sub + p_sub
    last = n_sfc * n_sub - 1
    k, nx, plane = vec_ref.shape

    lanes = raw.shape[-1]
    loads = [
        pltpu.make_async_copy(vec_ref.at[:, :, pl.ds(i * lanes, lanes)], raw.at[i], in_sem.at[i])
        for i in range(plane // lanes)
    ]
    loads.append(
        pltpu.make_async_copy(react_ref, react.at[pl.ds(8, nx)], in_sem.at[plane // lanes])
    )
    for load in loads:
        load.start()

    def device(index):
        return (lax.div(index, n_sub), lax.rem(index, n_sub))

    has_left, has_right = me > 0, me < last
    barrier = pltpu.get_barrier_semaphore()

    def greet(axis, count, mine):
        def one(i):
            pl.semaphore_signal(
                barrier, inc=1, device_id={axis: lax.rem(mine + i + 1, count)}, device_id_type=MESH
            )

        loop(count - 1, one)

    @pl.when(has_left)
    def _():
        pl.semaphore_signal(barrier, inc=1, device_id=device(me - 1), device_id_type=MESH)

    @pl.when(has_right)
    def _():
        pl.semaphore_signal(barrier, inc=1, device_id=device(me + 1), device_id_type=MESH)

    greet("sub", n_sub, p_sub)
    greet("sfc", n_sfc, p_sfc)

    for load in loads:
        load.wait()
    flats = [raw.at[i].reshape(k * nx, lanes) for i in range(plane // lanes)]

    def slab(x):
        return jnp.concatenate([flat[pl.ds(x, k, stride=nx), :] for flat in flats], axis=1)

    halo = width * k
    for i in range(width):
        send_l[pl.ds(i * k, k), :] = slab(i)
        send_r[pl.ds(i * k, k), :] = slab(nx - width + i)
    send_l[pl.ds(halo, 8), :] = react[pl.ds(8, 8), :]
    send_r[pl.ds(halo, 8), :] = react[pl.ds(nx, 8), :]
    for x in range(nx):
        fields[0, width + x] = slab(x)

    pl.semaphore_wait(
        barrier, (n_sub - 1) + (n_sfc - 1) + jnp.minimum(me, 1) + jnp.minimum(last - me, 1)
    )

    def to_left():
        return pltpu.make_async_remote_copy(
            src_ref=send_l, dst_ref=from_r, send_sem=halo_send.at[0], recv_sem=halo_recv.at[1],
            device_id=device(me - 1), device_id_type=MESH,
        )

    def to_right():
        return pltpu.make_async_remote_copy(
            src_ref=send_r, dst_ref=from_l, send_sem=halo_send.at[1], recv_sem=halo_recv.at[0],
            device_id=device(me + 1), device_id_type=MESH,
        )

    @pl.when(has_left)
    def _():
        to_left().start()

    @pl.when(has_right)
    def _():
        to_right().start()

    table = table_ref[...]

    def products(p, lo, hi):
        v = fields[p, width + lo : width + hi].reshape((hi - lo) * k, plane)
        a, b, c = split3(v)
        both = (
            jnp.dot(a, table, preferred_element_type=F32)
            + jnp.dot(b, table, preferred_element_type=F32)
            + jnp.dot(c, table, preferred_element_type=F32)
        )
        edges[p, width + lo : width + hi] = (both[:, :plane] * (1.0 / 432.0)).reshape(hi - lo, k, plane)
        own = both[:, plane:] * (1.0 / 108.0)
        gain = react[8 + lo : 8 + hi, :][:, None, :]
        fields[p + 1, width + lo : width + hi] = own.reshape(hi - lo, k, plane) + gain * v.reshape(hi - lo, k, plane)

    def combine(p, x):
        fields[p + 1, width + x] = (
            fields[p + 1, width + x] + edges[p, width + x - 1] + edges[p, width + x + 1]
        )

    for p in range(width):
        products(p, p, nx - p)
        for x in range(p + 1, nx - p - 1):
            combine(p, x)
    inner = gram_of([fields[width, width + x] for x in range(width, nx - width)])

    zero = jnp.zeros((halo + 8, plane), F32)

    @pl.when(has_left)
    def _():
        to_right_in = pltpu.make_async_remote_copy(
            src_ref=send_r, dst_ref=from_l, send_sem=halo_send.at[1], recv_sem=halo_recv.at[0],
            device_id=device(me - 1), device_id_type=MESH,
        )
        to_right_in.wait_recv()

    @pl.when(jnp.logical_not(has_left))
    def _():
        from_l[...] = zero

    @pl.when(has_right)
    def _():
        to_left_in = pltpu.make_async_remote_copy(
            src_ref=send_l, dst_ref=from_r, send_sem=halo_send.at[0], recv_sem=halo_recv.at[1],
            device_id=device(me + 1), device_id_type=MESH,
        )
        to_left_in.wait_recv()

    @pl.when(jnp.logical_not(has_right))
    def _():
        from_r[...] = zero

    for i in range(width):
        fields[0, i] = from_l[pl.ds(i * k, k), :]
        fields[0, width + nx + i] = from_r[pl.ds(i * k, k), :]
    react[pl.ds(0, 8), :] = from_l[pl.ds(halo, 8), :]
    react[pl.ds(8 + nx, 8), :] = from_r[pl.ds(halo, 8), :]

    keep_left = jnp.where(has_left, 1.0, 0.0).astype(F32)
    keep_right = jnp.where(has_right, 1.0, 0.0).astype(F32)
    for p in range(width):
        products(p, p - width, p)
        products(p, nx - p, nx - p + width)
        for x in range(p - width + 1, p + 1):
            combine(p, x)
            mirror = nx - 1 - x
            combine(p, mirror)
            if x < 0:
                fields[p + 1, width + x] = fields[p + 1, width + x] * keep_left
                fields[p + 1, width + mirror] = fields[p + 1, width + mirror] * keep_right

    outer_rows = list(range(width)) + list(range(nx - width, nx))
    gram = inner + gram_of([fields[width, width + x] for x in outer_rows])

    def reduce(gram, box_sub, ss, rs, box_sfc, sf, rf):
        part, sent_a = gather_sum("sub", box_sub, ss, rs, pack(gram))
        total, sent_b = gather_sum("sfc", box_sfc, sf, rf, part)
        return total, (sent_a, sent_b)

    total, sent1 = reduce(gram, box_sub1, ss1, rs1, box_sfc1, sf1, rf1)
    upper, inverse = eliminate(unpack(total))
    upper_ref[...] = upper
    parts = left_parts(inverse)
    for x in range(nx):
        q_ref[x] = left_apply(parts, fields[width, width + x])
    gram = gram_of([q_ref[x] for x in range(nx)])
    total, sent2 = reduce(gram, box_sub2, ss2, rs2, box_sfc2, sf2, rf2)
    gram_ref[...] = total

    for done in sent1 + sent2:
        done()

    @pl.when(has_left)
    def _():
        to_left().wait_send()

    @pl.when(has_right)
    def _():
        to_right().wait_send()


def last_kernel(scale, q_ref, upper_ref, gram_ref, basis_ref, out_upper_ref, wide, sems):
    nx, k, plane = q_ref.shape
    second, inverse = eliminate(unpack(gram_ref[...]))
    parts = left_parts(inverse * scale)
    pieces = wide.shape[0]
    flats = [wide.at[i].reshape(k * nx, LANES) for i in range(pieces)]
    copies = []
    for x in range(nx):
        slab = left_apply(parts, q_ref[x])
        for i in range(pieces):
            flats[i][pl.ds(x, k, stride=nx), :] = slab[:, i * LANES : (i + 1) * LANES]
        if x % 8 == 7:
            rows = pl.ds(x - 7, 8)
            for i in range(pieces):
                copy = pltpu.make_async_copy(
                    wide.at[i, :, rows, :],
                    basis_ref.at[:, rows, pl.ds(i * LANES, LANES)],
                    sems.at[x // 8, i],
                )
                copy.start()
                copies.append(copy)
    out_upper_ref[...] = jnp.dot(
        second, upper_ref[...], precision=lax.Precision.HIGHEST, preferred_element_type=F32
    ) * (1.0 / scale)
    for copy in copies:
        copy.wait()


def per_device(vectors, reaction):
    k, nx, plane = vectors.shape
    n_sfc, n_sub = lax.axis_size("sfc"), lax.axis_size("sub")
    table = jnp.asarray(plane_table(NY, NL), BF16)
    scale = math.sqrt(n_sfc * n_sub * nx * plane)
    vmem = pl.BlockSpec(memory_space=pltpu.VMEM)
    anywhere = pl.BlockSpec(memory_space=pl.ANY)
    dma = pltpu.SemaphoreType.DMA
    halo = POWERS * k + 8
    q, upper, gram = pl.pallas_call(
        main_kernel,
        out_shape=(
            jax.ShapeDtypeStruct((nx, k, plane), F32),
            jax.ShapeDtypeStruct((k, k), F32),
            jax.ShapeDtypeStruct((k // 2, 2 * k), F32),
        ),
        in_specs=[anywhere, anywhere, vmem],
        out_specs=(vmem, vmem, vmem),
        scratch_shapes=[
            pltpu.VMEM((plane // LANES, k, nx, LANES), F32),
            pltpu.VMEM((nx + 16, plane), F32),
            pltpu.VMEM((POWERS + 1, nx + 2 * POWERS, k, plane), F32),
            pltpu.VMEM((POWERS, nx + 2 * POWERS, k, plane), F32),
            pltpu.VMEM((halo, plane), F32),
            pltpu.VMEM((halo, plane), F32),
            pltpu.VMEM((halo, plane), F32),
            pltpu.VMEM((halo, plane), F32),
            pltpu.VMEM((n_sub, k // 2, 2 * k), F32),
            pltpu.VMEM((n_sfc, k // 2, 2 * k), F32),
            pltpu.VMEM((n_sub, k // 2, 2 * k), F32),
            pltpu.VMEM((n_sfc, k // 2, 2 * k), F32),
            dma((plane // LANES + 1,)),
            dma((2,)),
            dma((2,)),
            dma((n_sub,)),
            dma((n_sub,)),
            dma((n_sfc,)),
            dma((n_sfc,)),
            dma((n_sub,)),
            dma((n_sub,)),
            dma((n_sfc,)),
            dma((n_sfc,)),
        ],
        compiler_params=pltpu.CompilerParams(
            collective_id=0, has_side_effects=True, vmem_limit_bytes=48 * 1024 * 1024
        ),
        name="power_gram_factor",
    )(vectors, reaction, table)
    basis, upper = pl.pallas_call(
        functools.partial(last_kernel, scale),
        out_shape=(
            jax.ShapeDtypeStruct((k, nx, plane), F32),
            jax.ShapeDtypeStruct((k, k), F32),
        ),
        in_specs=[vmem, vmem, vmem],
        out_specs=(anywhere, vmem),
        scratch_shapes=[
            pltpu.VMEM((plane // LANES, k, nx, LANES), F32),
            dma((nx // 8, plane // LANES)),
        ],
        compiler_params=pltpu.CompilerParams(vmem_limit_bytes=32 * 1024 * 1024),
        name="second_factor",
    )(q, upper, gram)
    return basis, upper


def solution(mesh):
    placed = (P(None, ("sfc", "sub"), None), P(("sfc", "sub"), None))
    return jax.shard_map(
        per_device,
        mesh=mesh,
        in_specs=placed,
        out_specs=(P(None, ("sfc", "sub"), None), P()),
        check_vma=False,
    )
```

time: 153 us -> 42.4 us (0.28)
  blocking collectives: 86.2 us -> 0 us
  Pallas kernels: 0 us -> 38.6 us
  other arithmetic: 26.6 us -> 0 us
  starting transfers between devices: 16.2 us -> 0 us
  matrix products: 12.2 us -> 0 us
  waiting for transfers between devices: 7.62 us -> 0 us
    psum x2 -> x0, blocking collectives: 86.2 us -> none  [whole_factor(): total = lax.psum(gram, ('sfc', 'sub'))]
    pallas_call x0 -> x2, Pallas kernels: none -> 38.6 us  [the longest x1 33.6 us: per_device(): pl.pallas_call(main_kernel, out_shape=(jax.ShapeDtypeStruct((nx, k, plane...]
    another operation x10 -> x0, other arithmetic: 24.3 us -> none  [the longest x6 13.1 us: whole_factor(): return jnp.linalg.cholesky(total)]
    ppermute x6 -> x0, starting transfers between devices: 16.2 us -> none  [the longest x3 12.4 us: with_halo(): lax.ppermute(tail, axis, [(i, (i + 1) % count) for i in range(ends)])]
    dot_general x6 -> x0, matrix products: 10.1 us -> none  [the longest x3 5.98 us: plane_products(): jnp.einsum('kzp,pq->kzq', field, table, precision=lax.Precision.HIGHEST)]
    ppermute x6 -> x0, waiting for transfers between devices: 7.62 us -> none  [the longest x3 7.61 us: with_halo(): lax.ppermute(head, axis, [((i + 1) % count, i) for i in range(ends)])]
    another operation x2 -> x0, matrix products: 2.08 us -> none  [lower_solve(): return lax.linalg.triangular_solve(lower, block, left_side=True, lower=True)]
  transfers between devices with their start and end apart: 6 -> 0, of which waited for: 3 -> 0; matrix products, arithmetic and copies ran while one was open for 0% -> 0% of each run, Pallas kernels for 0% -> 0%
where the time goes in v1:
time: 42.4 us; the launch traced here: 42.1 us
  Pallas kernels  38.6 us (91%)
  local copies, waits for them, and re-layouts  2.88 us (7%)
  between operations  0.65 us (2%)
    pallas_call x1, Pallas kernels, per_device(): pl.pallas_call(main_kernel, out_shape=(jax.ShapeDtypeStruct((nx, k, plane...  33.6 us
    pallas_call x1, Pallas kernels, per_device(): pl.pallas_call(functools.partial(last_kernel, scale), out_shape=(jax.Shap...  5.05 us
    unnamed x6, local copies, waits for them, and re-layouts  2.88 us

profile of v1, /device:TPU:0, one launch (start us, length us, event | category | flops | bytes accessed | tf_op | source)
XLA Modules:
  0.0 42.1 jit_solution(852778622478951494)
XLA Ops:
  0.6 0.0 copy-start
  0.6 1.2 %copy-done = f32[64,16,256]{2,1,0:T(8,128)S(1)} copy-done((f32[64,16,256]{2,1,0:T(8,128)S(1)}, f32[64,16,256]{2,1,0:T(8,128)}, u32[]{:S(2)}) %copy-start) | copy-done | bytes 1048600
  1.9 0.0 copy-start.1
  1.9 0.9 %copy-done.1 = bf16[256,512]{1,0:T(8,128)(2,1)S(1)} copy-done((bf16[256,512]{1,0:T(8,128)(2,1)S(1)}, bf16[256,512]{1,0:T(8,128)(2,1)}, u32[]{:S(2)}) %copy-start.1) | copy-done | bytes 262168
  2.8 0.0 copy-start.2
  2.8 0.7 %copy-done.2 = f32[16,256]{1,0:T(8,128)S(1)} copy-done((f32[16,256]{1,0:T(8,128)S(1)}, f32[16,256]{1,0:T(8,128)}, u32[]{:S(2)}) %copy-start.2) | copy-done | bytes 16408
  3.5 33.6 %power_gram_factor.1 = (f32[16,64,256]{2,1,0:T(8,128)S(1)}, f32[64,64]{1,0:T(8,128)S(1)}, f32[32,128]{1,0:T(8,128)S(1)}) custom-call(f32[64,16,256]{2,1,0:T(8,128)S(1)} %copy-done, f32[16,256]{1,0:T(8,128)S(1)} %copy-done.2, bf16[256,512]{1,0:T(8,128)(2,1)S(1)} %copy-done.1), custom_call_target="tpu_custom_call" | custom-call | tf_op jit(solution)/shard_map/power_gram_factor/pallas_call | solution.py:378
  37.1 5.1 %second_factor.1 = (f32[64,16,256]{2,1,0:T(8,128)}, f32[64,64]{1,0:T(8,128)}) custom-call(f32[16,64,256]{2,1,0:T(8,128)S(1)} %get-tuple-element.5.q_ref, f32[64,64]{1,0:T(8,128)S(1)} %get-tuple-element.6.upper_ref, f32[32,128]{1,0:T(8,128)S(1)} %get-tuple-element.7.gram_ref), custom_call_target="tpu_custom_call" | custom-call | tf_op jit(solution)/shard_map/second_factor/pallas_call | solution.py:417
Async XLA Ops:
  0.6 1.2 %copy-start = (f32[64,16,256]{2,1,0:T(8,128)S(1)}, f32[64,16,256]{2,1,0:T(8,128)}, u32[]{:S(2)}) copy-start(f32[64,16,256]{2,1,0:T(8,128)} %vec_ref.1) | copy-start | bytes 3145732
  1.9 0.9 %copy-start.1 = (bf16[256,512]{1,0:T(8,128)(2,1)S(1)}, bf16[256,512]{1,0:T(8,128)(2,1)}, u32[]{:S(2)}) copy-start(bf16[256,512]{1,0:T(8,128)(2,1)} %constant.2.clone.table_ref) | copy-start | bytes 786436
  2.8 0.7 %copy-start.2 = (f32[16,256]{1,0:T(8,128)S(1)}, f32[16,256]{1,0:T(8,128)}, u32[]{:S(2)}) copy-start(f32[16,256]{1,0:T(8,128)} %react_ref.1) | copy-start | bytes 49156

commit v2 on v1

--- a/solution.py
+++ b/solution.py
@@ -16,8 +16,9 @@
 MESH = pl.DeviceIdType.MESH
 F32 = jnp.float32
 BF16 = jnp.bfloat16
-STEP = 4
+STEP = 16
 LANES = 128
+VMEM_ALL = 67043328
 
 
 def plane_table(across, layers):
@@ -101,25 +102,48 @@
     return upper, inverse
 
 
+def square(size):
+    rows = lax.broadcasted_iota(jnp.int32, (size, size), 0)
+    return rows, lax.broadcasted_iota(jnp.int32, (size, size), 1)
+
+
 def pack(gram):
     half = gram.shape[0] // 2
-    return jnp.concatenate([gram[:half], gram[half:]], axis=1)
+    rows, cols = square(half)
+    first, cross, second = gram[:half, :half], gram[:half, half:], gram[half:, half:]
+    tall = jnp.concatenate([jnp.where(rows >= cols, first, second), cross], axis=1)
+    diagonal = jnp.sum(jnp.where(rows == cols, second, 0.0), axis=0, keepdims=True)
+    wide = jnp.concatenate([tall[: half // 2], tall[half // 2 :]], axis=1)
+    rest = jnp.concatenate([diagonal, jnp.zeros((1, 3 * half), F32)], axis=1)
+    return jnp.concatenate([wide, rest], axis=0)
 
 
 def unpack(packed):
     k = packed.shape[1] // 2
-    return jnp.concatenate([packed[:, :k], packed[:, k:]], axis=0)
+    half = k // 2
+    rows, cols = square(half)
+    wide = packed[: half // 2]
+    tall = jnp.concatenate([wide[:, :k], wide[:, k:]], axis=0)
+    turned = tall.T
+    both, cross = tall[:, :half], tall[:, half:]
+    first = jnp.where(rows >= cols, both, turned[:half])
+    diagonal = packed[half // 2 : half // 2 + 1, :half]
+    second = jnp.where(rows < cols, both, jnp.where(rows > cols, turned[:half], diagonal))
+    return jnp.concatenate(
+        [jnp.concatenate([first, cross], axis=1), jnp.concatenate([turned[half:], second], axis=1)], axis=0
+    )
 
 
 def gather_sum(axis, box, send_sem, recv_sem, value):
     count = lax.axis_size(axis)
     me = lax.axis_index(axis)
-    box[me] = value
+    sent = pl.ds(0, value.shape[0])
+    box[me, sent] = value
 
     def copy(i, slot, target):
         return pltpu.make_async_remote_copy(
-            src_ref=box.at[slot],
-            dst_ref=box.at[slot],
+            src_ref=box.at[slot, sent],
+            dst_ref=box.at[slot, sent],
             send_sem=send_sem.at[i],
             recv_sem=recv_sem.at[slot],
             device_id={axis: target},
@@ -133,25 +157,25 @@
         other = lax.rem(me + i + 1, count)
         copy(i, other, other).wait_recv()
 
-    def sent(i):
+    def finish(i):
         copy(i, me, lax.rem(me + i + 1, count)).wait_send()
 
     loop(count - 1, start)
     loop(count - 1, take)
     if count <= 16:
-        total = box[0]
+        total = box[0, sent]
         for i in range(1, count):
-            total = total + box[i]
+            total = total + box[i, sent]
     else:
-        total = lax.fori_loop(1, count, lambda i, t: t + box[i], box[0])
-    return total, lambda: loop(count - 1, sent)
+        total = lax.fori_loop(1, count, lambda i, t: t + box[i, sent], box[0, sent])
+    return total, lambda: loop(count - 1, finish)
 
 
 def main_kernel(
     vec_ref, react_ref, table_ref, q_ref, upper_ref, gram_ref,
-    raw, react, fields, edges, send_l, send_r, from_l, from_r,
+    raw, react, coefficients, fields, edges, send_l, send_r, from_l, from_r,
     box_sub1, box_sfc1, box_sub2, box_sfc2,
-    in_sem, halo_send, halo_recv,
+    upper_buf, in_sem, out_sem, halo_send, halo_recv,
     ss1, rs1, sf1, rf1, ss2, rs2, sf2, rf2,
 ):
     width = POWERS
@@ -169,6 +193,7 @@
     loads.append(
         pltpu.make_async_copy(react_ref, react.at[pl.ds(8, nx)], in_sem.at[plane // lanes])
     )
+    loads.append(pltpu.make_async_copy(table_ref, coefficients, in_sem.at[plane // lanes + 1]))
     for load in loads:
         load.start()
 
@@ -197,7 +222,7 @@
     greet("sub", n_sub, p_sub)
     greet("sfc", n_sfc, p_sfc)
 
-    for load in loads:
+    for load in loads[:-1]:
         load.wait()
     flats = [raw.at[i].reshape(k * nx, lanes) for i in range(plane // lanes)]
 
@@ -237,7 +262,8 @@
     def _():
         to_right().start()
 
-    table = table_ref[...]
+    loads[-1].wait()
+    table = coefficients[...]
 
     def products(p, lo, hi):
         v = fields[p, width + lo : width + hi].reshape((hi - lo) * k, plane)
@@ -318,14 +344,23 @@
 
     total, sent1 = reduce(gram, box_sub1, ss1, rs1, box_sfc1, sf1, rf1)
     upper, inverse = eliminate(unpack(total))
-    upper_ref[...] = upper
+    upper_buf[...] = upper
     parts = left_parts(inverse)
     for x in range(nx):
-        q_ref[x] = left_apply(parts, fields[width, width + x])
-    gram = gram_of([q_ref[x] for x in range(nx)])
+        fields[0, width + x] = left_apply(parts, fields[width, width + x])
+    gram = gram_of([fields[0, width + x] for x in range(nx)])
+    stores = [
+        pltpu.make_async_copy(fields.at[0, pl.ds(width, nx)], q_ref, out_sem.at[0]),
+        pltpu.make_async_copy(upper_buf, upper_ref, out_sem.at[1]),
+    ]
+    for store in stores:
+        store.start()
     total, sent2 = reduce(gram, box_sub2, ss2, rs2, box_sfc2, sf2, rf2)
-    gram_ref[...] = total
-
+    short = gram_ref.shape[0] - total.shape[0]
+    gram_ref[...] = jnp.concatenate([total, jnp.zeros((short, total.shape[1]), F32)], axis=0)
+
+    for done in stores:
+        done.wait()
     for done in sent1 + sent2:
         done()
 
@@ -338,10 +373,18 @@
         to_right().wait_send()
 
 
-def last_kernel(scale, q_ref, upper_ref, gram_ref, basis_ref, out_upper_ref, wide, sems):
-    nx, k, plane = q_ref.shape
+def last_kernel(scale, q_hbm, upper_hbm, gram_ref, basis_ref, out_upper_ref, q_ref, upper_ref, wide, in_sem, sems):
+    nx, k, plane = q_hbm.shape
+    loads = [
+        pltpu.make_async_copy(q_hbm, q_ref, in_sem.at[0]),
+        pltpu.make_async_copy(upper_hbm, upper_ref, in_sem.at[1]),
+    ]
+    for load in loads:
+        load.start()
     second, inverse = eliminate(unpack(gram_ref[...]))
     parts = left_parts(inverse * scale)
+    for load in loads:
+        load.wait()
     pieces = wide.shape[0]
     flats = [wide.at[i].reshape(k * nx, LANES) for i in range(pieces)]
     copies = []
@@ -372,32 +415,37 @@
     table = jnp.asarray(plane_table(NY, NL), BF16)
     scale = math.sqrt(n_sfc * n_sub * nx * plane)
     vmem = pl.BlockSpec(memory_space=pltpu.VMEM)
-    anywhere = pl.BlockSpec(memory_space=pl.ANY)
+    hbm = pl.BlockSpec(memory_space=pltpu.HBM)
     dma = pltpu.SemaphoreType.DMA
     halo = POWERS * k + 8
+    tall = (k // 4 + 8) // 8 * 8
+    room = 4 * tall * 2 * k + 2048
     q, upper, gram = pl.pallas_call(
         main_kernel,
         out_shape=(
             jax.ShapeDtypeStruct((nx, k, plane), F32),
             jax.ShapeDtypeStruct((k, k), F32),
-            jax.ShapeDtypeStruct((k // 2, 2 * k), F32),
+            jax.ShapeDtypeStruct((tall, 2 * k), F32),
         ),
-        in_specs=[anywhere, anywhere, vmem],
-        out_specs=(vmem, vmem, vmem),
+        in_specs=[hbm, hbm, hbm],
+        out_specs=(hbm, hbm, vmem),
         scratch_shapes=[
             pltpu.VMEM((plane // LANES, k, nx, LANES), F32),
             pltpu.VMEM((nx + 16, plane), F32),
+            pltpu.VMEM(table.shape, BF16),
             pltpu.VMEM((POWERS + 1, nx + 2 * POWERS, k, plane), F32),
             pltpu.VMEM((POWERS, nx + 2 * POWERS, k, plane), F32),
             pltpu.VMEM((halo, plane), F32),
             pltpu.VMEM((halo, plane), F32),
             pltpu.VMEM((halo, plane), F32),
             pltpu.VMEM((halo, plane), F32),
-            pltpu.VMEM((n_sub, k // 2, 2 * k), F32),
-            pltpu.VMEM((n_sfc, k // 2, 2 * k), F32),
-            pltpu.VMEM((n_sub, k // 2, 2 * k), F32),
-            pltpu.VMEM((n_sfc, k // 2, 2 * k), F32),
-            dma((plane // LANES + 1,)),
+            pltpu.VMEM((n_sub, tall, 2 * k), F32),
+            pltpu.VMEM((n_sfc, tall, 2 * k), F32),
+            pltpu.VMEM((n_sub, tall, 2 * k), F32),
+            pltpu.VMEM((n_sfc, tall, 2 * k), F32),
+            pltpu.VMEM((k, k), F32),
+            dma((plane // LANES + 2,)),
+            dma((2,)),
             dma((2,)),
             dma((2,)),
             dma((n_sub,)),
@@ -410,7 +458,7 @@
             dma((n_sfc,)),
         ],
         compiler_params=pltpu.CompilerParams(
-            collective_id=0, has_side_effects=True, vmem_limit_bytes=48 * 1024 * 1024
+            collective_id=0, has_side_effects=True, vmem_limit_bytes=VMEM_ALL - room
         ),
         name="power_gram_factor",
     )(vectors, reaction, table)
@@ -420,13 +468,16 @@
             jax.ShapeDtypeStruct((k, nx, plane), F32),
             jax.ShapeDtypeStruct((k, k), F32),
         ),
-        in_specs=[vmem, vmem, vmem],
-        out_specs=(anywhere, vmem),
+        in_specs=[hbm, hbm, vmem],
+        out_specs=(hbm, vmem),
         scratch_shapes=[
+            pltpu.VMEM((nx, k, plane), F32),
+            pltpu.VMEM((k, k), F32),
             pltpu.VMEM((plane // LANES, k, nx, LANES), F32),
+            dma((2,)),
             dma((nx // 8, plane // LANES)),
         ],
-        compiler_params=pltpu.CompilerParams(vmem_limit_bytes=32 * 1024 * 1024),
+        compiler_params=pltpu.CompilerParams(vmem_limit_bytes=VMEM_ALL - room),
         name="second_factor",
     )(q, upper, gram)
     return basis, upper

time: 42.4 us -> 38.1 us (0.90)
  local copies, waits for them, and re-layouts: 2.88 us -> 0 us
  Pallas kernels: 38.6 us -> 37.2 us
    unnamed x6 -> x0, local copies, waits for them, and re-layouts: 2.88 us -> none
    pallas_call x1, Pallas kernels: 33.6 us -> 31.7 us  [per_device(): pl.pallas_call(main_kernel, out_shape=(jax.ShapeDtypeStruct((nx, k, plane...]
where the time goes in v2:
time: 38.1 us; the launch traced here: 37.8 us
  Pallas kernels  37.2 us (98%)
  between operations  0.64 us (2%)
    pallas_call x1, Pallas kernels, per_device(): pl.pallas_call(main_kernel, out_shape=(jax.ShapeDtypeStruct((nx, k, plane...  31.7 us
    pallas_call x1, Pallas kernels, per_device(): pl.pallas_call(functools.partial(last_kernel, scale), out_shape=(jax.Shap...  5.46 us

profile of v2, /device:TPU:0, one launch (start us, length us, event | category | flops | bytes accessed | tf_op | source)
XLA Modules:
  0.0 37.8 jit_solution(4999730124993725897)
XLA Ops:
  0.6 31.7 %power_gram_factor.1 = (f32[16,64,256]{2,1,0:T(8,128)}, f32[64,64]{1,0:T(8,128)}, f32[24,128]{1,0:T(8,128)}) custom-call(f32[64,16,256]{2,1,0:T(8,128)} %vec_ref.1, f32[16,256]{1,0:T(8,128)} %react_ref.1, bf16[256,512]{1,0:T(8,128)(2,1)} %constant.2.clone.table_ref), custom_call_target="tpu_custom_call" | custom-call | tf_op jit(solution)/shard_map/power_gram_factor/pallas_call | solution.py:423
  32.4 5.5 %second_factor.1 = (f32[64,16,256]{2,1,0:T(8,128)}, f32[64,64]{1,0:T(8,128)}) custom-call(f32[16,64,256]{2,1,0:T(8,128)} %get-tuple-element.5.q_hbm, f32[64,64]{1,0:T(8,128)} %get-tuple-element.6.upper_hbm, f32[24,128]{1,0:T(8,128)} %get-tuple-element.7.gram_ref), custom_call_target="tpu_custom_call" | custom-call | tf_op jit(solution)/shard_map/second_factor/pallas_call | solution.py:465

commit v3 on v2

--- a/solution.py
+++ b/solution.py
@@ -264,19 +264,21 @@
 
     loads[-1].wait()
     table = coefficients[...]
-
-    def products(p, lo, hi):
-        v = fields[p, width + lo : width + hi].reshape((hi - lo) * k, plane)
-        a, b, c = split3(v)
-        both = (
-            jnp.dot(a, table, preferred_element_type=F32)
-            + jnp.dot(b, table, preferred_element_type=F32)
-            + jnp.dot(c, table, preferred_element_type=F32)
-        )
-        edges[p, width + lo : width + hi] = (both[:, :plane] * (1.0 / 432.0)).reshape(hi - lo, k, plane)
-        own = both[:, plane:] * (1.0 / 108.0)
-        gain = react[8 + lo : 8 + hi, :][:, None, :]
-        fields[p + 1, width + lo : width + hi] = own.reshape(hi - lo, k, plane) + gain * v.reshape(hi - lo, k, plane)
+    tables = jnp.concatenate([table, table, table], axis=0)
+
+    def products(p, *spans):
+        slabs = [fields[p, width + x] for lo, hi in spans for x in range(lo, hi)]
+        parts = [split3(v) for v in slabs]
+        wide = jnp.concatenate([jnp.concatenate(part, axis=1) for part in parts], axis=0)
+        both = jnp.dot(wide, tables, preferred_element_type=F32)
+        row = 0
+        for lo, hi in spans:
+            for x in range(lo, hi):
+                piece = both[row * k : (row + 1) * k]
+                edges[p, width + x] = piece[:, :plane] * (1.0 / 432.0)
+                own = piece[:, plane:] * (1.0 / 108.0)
+                fields[p + 1, width + x] = own + react[8 + x : 9 + x, :] * slabs[row]
+                row += 1
 
     def combine(p, x):
         fields[p + 1, width + x] = (
@@ -284,7 +286,7 @@
         )
 
     for p in range(width):
-        products(p, p, nx - p)
+        products(p, (p, nx - p))
         for x in range(p + 1, nx - p - 1):
             combine(p, x)
     inner = gram_of([fields[width, width + x] for x in range(width, nx - width)])
@@ -324,8 +326,7 @@
     keep_left = jnp.where(has_left, 1.0, 0.0).astype(F32)
     keep_right = jnp.where(has_right, 1.0, 0.0).astype(F32)
     for p in range(width):
-        products(p, p - width, p)
-        products(p, nx - p, nx - p + width)
+        products(p, (p - width, p), (nx - p, nx - p + width))
         for x in range(p - width + 1, p + 1):
             combine(p, x)
             mirror = nx - 1 - x

time: 38.1 us -> 38.3 us (level)
  no operation moved by 1% of the time
where the time goes in v3:
time: 38.3 us; the launch traced here: 38.1 us
  Pallas kernels  37.4 us (98%)
  between operations  0.64 us (2%)
    pallas_call x1, Pallas kernels, per_device(): pl.pallas_call(main_kernel, out_shape=(jax.ShapeDtypeStruct((nx, k, plane...  32 us
    pallas_call x1, Pallas kernels, per_device(): pl.pallas_call(functools.partial(last_kernel, scale), out_shape=(jax.Shap...  5.46 us

profile of v3, /device:TPU:0, one launch (start us, length us, event | category | flops | bytes accessed | tf_op | source)
XLA Modules:
  0.0 38.1 jit_solution(17697287552974532044)
XLA Ops:
  0.6 32.0 %power_gram_factor.1 = (f32[16,64,256]{2,1,0:T(8,128)}, f32[64,64]{1,0:T(8,128)}, f32[24,128]{1,0:T(8,128)}) custom-call(f32[64,16,256]{2,1,0:T(8,128)} %vec_ref.1, f32[16,256]{1,0:T(8,128)} %react_ref.1, bf16[256,512]{1,0:T(8,128)(2,1)} %constant.2.clone.table_ref), custom_call_target="tpu_custom_call" | custom-call | tf_op jit(solution)/shard_map/power_gram_factor/pallas_call | solution.py:424
  32.6 5.5 %second_factor.1 = (f32[64,16,256]{2,1,0:T(8,128)}, f32[64,64]{1,0:T(8,128)}) custom-call(f32[16,64,256]{2,1,0:T(8,128)} %get-tuple-element.5.q_hbm, f32[64,64]{1,0:T(8,128)} %get-tuple-element.6.upper_hbm, f32[24,128]{1,0:T(8,128)} %get-tuple-element.7.gram_ref), custom_call_target="tpu_custom_call" | custom-call | tf_op jit(solution)/shard_map/second_factor/pallas_call | solution.py:466
